TPU v7x, 32 devices: a whole 2x2x4 slice. The times are simulated.
32 devices in a mesh: island: 4 (over z), shard: 8 (over y, x, core).
Axes of the slice: x: 2, y: 2, z: 4, core: 2. Of those that a mesh axis runs over, the one named last changes fastest.
Arguments:
- weight_master: float32 [4096, 4096], P('island', 'shard'), may hold values from -6 to 6
- gain_master: float32 [4096], P(('shard', 'island')), may hold values from 0.5 to 1.5
- weight_moment: float32 [4096, 4096], P('island', 'shard'), may hold values from -0.3 to 0.3
- gain_moment: float32 [4096], P(('shard', 'island')), may hold values from -0.3 to 0.3
- attended: bfloat16 [4, 2, 768, 4096], P('island', None, 'shard'), may hold values from -6 to 6
- stream: bfloat16 [4, 2, 768, 4096], P('island', None, None, 'shard'), may hold values from -6 to 6
- targets: bfloat16 [4, 2, 768, 4096], P('island', None, None, 'shard'), may hold values from -6 to 6
Outputs:
- weight_updated: float32 [4096, 4096], P('island', 'shard')
- gain_updated: float32 [4096], P(('shard', 'island'))
- weight_velocity: float32 [4096, 4096], P('island', 'shard')
- gain_velocity: float32 [4096], P(('shard', 'island'))
All inputs are finite; a program needn't handle non-finite values.
Results may differ from a plain program's by a relative error of at most 0.0066.
Values may be sent and summed in bfloat16 or wider, within the bound.
A program may use at most 192 MiB of HBM per device.

v0:
```python
import jax
import jax.numpy as jnp
from jax import lax
from jax.sharding import PartitionSpec as P

D = 4096
STEPS = 2


norm_epsilon = 1e-05
inner_rate = 0.05
beta_one = 0.9
beta_two = 0.95
adam_epsilon = 0.3
decay_rate = 0.1
outer_rate = 0.7
outer_momentum = 0.9


def optimizer_update(param, gradient, first, second, number, decay):
    first = beta_one * first + (1.0 - beta_one) * gradient
    second = beta_two * second + (1.0 - beta_two) * gradient * gradient
    first_hat = first / (1.0 - beta_one**number)
    second_hat = second / (1.0 - beta_two**number)
    param = param - inner_rate * (first_hat / (jnp.sqrt(second_hat) + adam_epsilon) + decay * param)
    return (param, first, second)


def per_device(weight_master, gain_master, weight_moment, gain_moment, attended, stream, targets):
    islands = lax.axis_size("island")
    width_scale = D ** (-0.5)
    starts = (
        lax.all_gather(weight_master.astype(jnp.bfloat16), "island", axis=0, tiled=True),
        lax.all_gather(gain_master.astype(jnp.bfloat16), "island", axis=0, tiled=True),
    )
    weight_anchor = starts[0].astype(jnp.float32)
    gain_anchor = starts[1].astype(jnp.float32)
    weight = weight_anchor
    gain = gain_anchor
    weight_first = jnp.zeros_like(weight)
    weight_second = jnp.zeros_like(weight)
    gain_first = jnp.zeros_like(gain)
    gain_second = jnp.zeros_like(gain)
    for inner_step in range(STEPS):
        number = inner_step + 1
        rows_full = lax.all_gather(attended[0][inner_step], "shard", axis=0, tiled=True)
        weight_low = weight.astype(jnp.bfloat16)
        projected = jnp.dot(rows_full, weight_low, preferred_element_type=jnp.float32) * width_scale
        residual = stream[0][inner_step].astype(jnp.float32) + projected
        squares = lax.psum(jnp.sum(residual * residual, axis=1), "shard")
        inverse = lax.rsqrt(squares / D + norm_epsilon)[:, None]
        normed = residual * inverse * gain
        loss_low = (normed - targets[0][inner_step].astype(jnp.float32)).astype(jnp.bfloat16)
        loss_grad = lax.optimization_barrier(loss_low).astype(jnp.float32)
        scaled = loss_grad * gain
        slope = lax.psum(jnp.sum(scaled * residual, axis=1), "shard")[:, None]
        residual_grad = (
            inverse * scaled - residual * inverse * inverse * inverse * slope / D
        ).astype(jnp.bfloat16)
        weight_grad = (
            jnp.einsum("td,tf->df", rows_full, residual_grad, preferred_element_type=jnp.float32)
            * width_scale
        )
        gain_grad = jnp.sum(loss_grad * residual * inverse, axis=0)
        weight, weight_first, weight_second = optimizer_update(
            weight, weight_grad, weight_first, weight_second, number, decay_rate
        )
        gain, gain_first, gain_second = optimizer_update(
            gain, gain_grad, gain_first, gain_second, number, 0.0
        )
    weight_summed, gain_summed = (
        lax.psum_scatter(weight_anchor - weight, "island", scatter_dimension=0, tiled=True),
        lax.psum_scatter(gain_anchor - gain, "island", scatter_dimension=0, tiled=True),
    )
    weight_pseudo = weight_summed / islands
    gain_pseudo = gain_summed / islands
    weight_velocity = outer_momentum * weight_moment + weight_pseudo
    gain_velocity = outer_momentum * gain_moment + gain_pseudo
    weight_updated = weight_master - outer_rate * (weight_pseudo + outer_momentum * weight_velocity)
    gain_updated = gain_master - outer_rate * (gain_pseudo + outer_momentum * gain_velocity)
    return (weight_updated, gain_updated, weight_velocity, gain_velocity)


def solution(mesh):
    placed = (
        P("island", "shard"),
        P(("shard", "island")),
        P("island", "shard"),
        P(("shard", "island")),
        P("island", None, "shard", None),
        P("island", None, None, "shard"),
        P("island", None, None, "shard"),
    )
    return jax.shard_map(
        per_device,
        mesh=mesh,
        in_specs=placed,
        out_specs=(
            P("island", "shard"),
            P(("shard", "island")),
            P("island", "shard"),
            P(("shard", "island")),
        ),
        check_vma=False,
    )
```

profile of v0, /device:TPU:8, one launch (start us, length us, event | category | flops | bytes accessed | tf_op | source)
XLA Modules:
  0.0 414.4 jit_solution(13585546172101198673)
XLA Ops:
  7.2 0.0 all-gather.7.cloned.1.call-start
  7.2 1.9 copy.26
  9.1 1.1 convert_element_type.58
  10.3 0.0 all-gather.7.cloned.1.call-update
  10.3 0.0 all-gather.9.cloned.1.call-start
  10.4 2.7 fusion.69
  13.0 0.0 all-gather.9.cloned.1.call-update
  13.0 0.0 all-gather.11.cloned.1.call-start
  13.1 0.7 all-gather.11.cloned.1.call-update
  13.8 0.0 copy-start.5
  13.8 0.0 reduce-scatter.2.cloned.1.call-start
  13.8 2.4 fusion.68
  16.2 2.3 copy.29
  18.5 8.9 %all-gather.2 = bf16[4,1,128]{2,1,0:T(2,128)(2,1)S(1)} all-gather(bf16[1,1,128]{2,1,0:T(2,128)(2,1)S(1)} %convert_bitcast_fusion), channel_id=1, replica_groups=mesh['island'=4,'shard'=8] {'island'}, dimensions={0}, use_global_device_ids=true | all-gather | bytes 1280 | tf_op jit(solution)/shard_map/all_gather | solution.py:34
  27.4 2.7 fusion.67
  30.1 2.3 copy.30
  32.4 1.2 copy.31
  33.6 1.4 copy.32
  35.0 54.7 %all-gather.7.cloned.1.call-done = bf16[4096,512]{0,1:T(8,128)(2,1)} async-done(((bf16[1024,512]{0,1:T(8,128)(2,1)}), bf16[4096,512]{0,1:T(8,128)(2,1)}) %all-gather.7.cloned.1.call-update) | async-done | bytes 4194320 | tf_op jit(solution)/shard_map/all_gather | solution.py:33
  89.7 48.4 %all-gather.9.cloned.1.call-done = bf16[1,1,768,4096]{3,2,1,0:T(8,128)(2,1)} async-done(((bf16[1,1,96,4096]{3,2,1,0:T(8,128)(2,1)}), bf16[1,1,768,4096]{3,2,1,0:T(8,128)(2,1)}) %all-gather.9.cloned.1.call-update) | async-done | bytes 6291472 | tf_op jit(solution)/shard_map/all_gather | solution.py:46
  138.1 8.8 %multiply_reduce_fusion.1 = (f32[768]{0:T(1024)S(1)}, f32[768,512]{0,1:T(8,128)}) fusion(bf16[4096,512]{0,1:T(8,128)(2,1)} %all-gather.7.cloned.1.call-done, bf16[1,1,768,4096]{3,2,1,0:T(8,128)(2,1)} %all-gather.9.cloned.1.call-done, bf16[1,1,768,512]{2,3,1,0:T(8,128)(2,1)} %copy.29), kind=kOutput, calls=%fused_computation.51 | convolution fusion | flops 3223190784 | bytes 12848128 | tf_op jit(solution)/shard_map/dot_general | solution.py:48
  146.9 13.7 %psum.28 = f32[768]{0:T(1024)S(1)} all-reduce(f32[768]{0:T(1024)S(1)} %get-tuple-element.26), channel_id=1, replica_groups=mesh['island'=4,'shard'=8] {'shard'}, use_global_device_ids=true, to_apply=%region_1.0 | all-reduce | flops 768 | bytes 6144 | tf_op jit(solution)/shard_map/psum | solution.py:50
  160.7 2.0 fusion.33
  162.7 0.1 copy-done.2
  162.8 0.6 fusion.29
  163.4 0.3 copy-done.4
  163.7 12.7 %psum.29 = f32[768]{0:T(1024)S(1)} all-reduce(f32[768]{0:T(1024)S(1)} %get-tuple-element.15), channel_id=1, replica_groups=mesh['island'=4,'shard'=8] {'shard'}, use_global_device_ids=true, to_apply=%region_3.0 | all-reduce | flops 768 | bytes 6144 | tf_op jit(solution)/shard_map/psum | solution.py:56
  176.4 10.5 %fusion.13 = f32[512,4096]{1,0:T(8,128)} fusion(bf16[1,1,768,4096]{3,2,1,0:T(8,128)(2,1)} %all-gather.9.cloned.1.call-done, bf16[768,512]{0,1:T(8,128)(2,1)} %copy-done.4, f32[768,512]{0,1:T(8,128)} %get-tuple-element.27, f32[768]{0:T(1024)S(1)} %psum.29, f32[512]{0:T(512)S(1)} %bitcast.94, f32[768]{0:T(1024)S(1)} %add_rsqrt_fusion.1), kind=kOutput, calls=%fused_computation.19 | convolution fusion | flops 3225157632 | bytes 17047552 | tf_op jit(solution)/shard_map/td,tf->df/dot_general | solution.py:61
  186.9 16.5 %multiply_reduce_fusion = (f32[768]{0:T(1024)S(1)}, f32[768,512]{0,1:T(8,128)}) fusion(bf16[1,1,768,4096]{3,2,1,0:T(8,128)(2,1)} %all-gather.11.cloned.1.call-done, f32[512,4096]{1,0:T(8,128)} %fusion.13, bf16[4096,512]{0,1:T(8,128)(2,1)} %all-gather.7.cloned.1.call-done, bf16[1,1,768,512]{2,3,1,0:T(8,128)(2,1)} %copy.31), kind=kOutput, calls=%fused_computation.50 | convolution fusion | flops 3248356608 | bytes 21236736 | tf_op jit(solution)/shard_map/dot_general | solution.py:48
  203.4 12.5 %psum.30 = f32[768]{0:T(1024)S(1)} all-reduce(f32[768]{0:T(1024)S(1)} %get-tuple-element.28), channel_id=1, replica_groups=mesh['island'=4,'shard'=8] {'shard'}, use_global_device_ids=true, to_apply=%region_5.0 | all-reduce | flops 768 | bytes 6144 | tf_op jit(solution)/shard_map/psum | solution.py:50
  215.9 1.8 fusion.32
  217.8 0.0 copy-done.1
  217.8 0.6 fusion.31
  218.4 0.2 copy-done.3
  218.7 12.0 %psum.31 = f32[768]{0:T(1024)S(1)} all-reduce(f32[768]{0:T(1024)S(1)} %get-tuple-element.13), channel_id=1, replica_groups=mesh['island'=4,'shard'=8] {'shard'}, use_global_device_ids=true, to_apply=%region_8.0 | all-reduce | flops 768 | bytes 6144 | tf_op jit(solution)/shard_map/psum | solution.py:56
  230.7 22.3 %convert_subtract_fusion = f32[4096,512]{0,1:T(8,128)} fusion(bf16[4096,512]{0,1:T(8,128)(2,1)} %all-gather.7.cloned.1.call-done, f32[512,4096]{1,0:T(8,128)} %fusion.13, bf16[1,1,768,4096]{3,2,1,0:T(8,128)(2,1)} %all-gather.11.cloned.1.call-done, bf16[768,512]{0,1:T(8,128)(2,1)} %copy-done.3, f32[768,512]{0,1:T(8,128)} %get-tuple-element.29, ...), kind=kOutput, calls=%fused_computation | convolution fusion | flops 3283877888 | bytes 29630464 | tf_op jit(solution)/shard_map/td,tf->df/dot_general | solution.py:61
  252.9 0.0 reduce-scatter.2.cloned.1.call-update
  253.0 0.0 copy-start.7
  253.0 0.0 copy-start.6
  253.0 2.9 copy.25
  255.9 0.6 dynamic-slice
  257.1 11.1 %all-reduce = f32[512]{0:T(512)S(1)} all-reduce(f32[512]{0:T(512)S(1)} %subtract_subtract_fusion), channel_id=5, replica_groups=mesh['island'=4,'shard'=8] {'island'}, use_global_device_ids=true, to_apply=%region_11.0.clone | all-reduce | flops 512 | bytes 4096
  268.2 0.6 multiply_subtract_fusion.2
  268.8 128.7 %reduce-scatter.2.cloned.1.call-done = f32[1024,512]{0,1:T(8,128)} async-done(((f32[4096,512]{0,1:T(8,128)}), f32[1024,512]{0,1:T(8,128)}) %reduce-scatter.2.cloned.1.call-update) | async-done | bytes 2097168 | tf_op jit(solution)/shard_map/reduce_scatter | solution.py:72
  397.6 5.5 %multiply_add_fusion = (f32[1024,512]{0,1:T(8,128)}, f32[1024,512]{0,1:T(8,128)}) fusion(f32[1024,512]{0,1:T(8,128)} %copy.25, f32[1024,512]{0,1:T(8,128)} %reduce-scatter.2.cloned.1.call-done, f32[1024,512]{0,1:T(8,128)S(1)} %copy.26), kind=kLoop, calls=%fused_computation.25 | loop fusion | flops 3670016 | bytes 10485760 | tf_op jit(solution)/shard_map/add | solution.py:77
  403.1 3.0 copy.27
  406.1 0.0 copy-done
  406.1 1.8 copy.28
  (15 shorter events, 0.1 us)
Async XLA Ops:
  7.2 82.6 %all-gather.7.cloned.1.call-start = ((), (), s32[]{:S(2)}) async-start(), calls=%async_computation.1 | async-start | bytes 5242880 | tf_op jit(solution)/shard_map/all_gather | solution.py:33
  10.3 127.8 %all-gather.9.cloned.1.call-start = ((), (), s32[]{:S(2)}) async-start(), calls=%async_computation.3 | async-start | bytes 7077888 | tf_op jit(solution)/shard_map/all_gather | solution.py:46
  13.0 173.9 %all-gather.11.cloned.1.call-start = ((), (), s32[]{:S(2)}) async-start(), calls=%async_computation.4 | async-start | bytes 7077888 | tf_op jit(solution)/shard_map/all_gather | solution.py:46
  13.8 4.7 %copy-start.5 = (f32[128]{0:T(128)S(1)}, f32[128]{0:T(128)}, u32[]{:S(2)}) copy-start(f32[128]{0:T(128)} %param.8) | copy-start | bytes 1540
  13.8 383.8 %reduce-scatter.2.cloned.1.call-start = ((), (), s32[]{:S(2)}) async-start(), calls=%async_computation.2 | async-start | bytes 10485760 | tf_op jit(solution)/shard_map/reduce_scatter | solution.py:72
  160.7 2.1 copy-start.2
  162.8 0.9 copy-start.4
  215.9 1.9 copy-start.1
  217.8 0.9 copy-start.3
  253.0 2.9 copy-start.7
  253.0 15.3 %copy-start.6 = (f32[128]{0:T(128)S(1)}, f32[128]{0:T(128)}, u32[]{:S(2)}) copy-start(f32[128]{0:T(128)} %param.10) | copy-start | bytes 1540
  403.0 3.0 copy-start
Sparse Core Ops, SparseCore 0:
  10.4 79.2 all-gather.6
  91.6 46.4 all-gather.8
  140.6 45.6 all-gather.10
  253.1 144.4 reduce-scatter.1
where the time goes:
time: 417 us; the launch traced here: 414 us
  waiting for transfers between devices  233 us (56%)
  blocking collectives  70.9 us (17%)
  matrix products  58.1 us (14%)
  local copies, waits for them, and re-layouts  25.8 us (6%)
  between operations  14.5 us (3%)
  other arithmetic  12.3 us (3%)
    reduce_scatter x1, waiting for transfers between devices, per_device(): lax.psum_scatter(weight_anchor - weight, 'island', scatter_dimension=0, t...  129 us
    all_gather x1, waiting for transfers between devices, per_device(): lax.all_gather(weight_master.astype(jnp.bfloat16), 'island', axis=0, tile...  54.7 us
    all_gather x2, waiting for transfers between devices, per_device(): lax.all_gather(attended[0][inner_step], 'shard', axis=0, tiled=True)  48.4 us
    dot_general x2, matrix products, per_device(): jnp.einsum('td,tf->df', rows_full, residual_grad, preferred_element_type=...  32.8 us
    psum x2, blocking collectives, per_device(): squares = lax.psum(jnp.sum(residual * residual, axis=1), 'shard')  26.2 us
    dot_general x2, matrix products, per_device(): jnp.dot(rows_full, weight_low, preferred_element_type=jnp.float32)  25.3 us
    psum x2, blocking collectives, per_device(): slope = lax.psum(jnp.sum(scaled * residual, axis=1), 'shard')[:, None]  24.7 us
    unnamed x25, local copies, waits for them, and re-layouts  18.1 us
  transfers between devices with their start and end apart: 4, of which 3 were waited for; matrix products, arithmetic and copies ran while one was open for 10% of the time, Pallas kernels for 0%

commit v1 on v0

v1 whole, which is shorter than its diff:
```python
import functools

import jax
import jax.numpy as jnp
from jax import lax
from jax.experimental import pallas as pl
from jax.experimental.pallas import tpu as pltpu
from jax.sharding import PartitionSpec as P

norm_epsilon = 1e-05
inner_rate = 0.05
beta_one = 0.9
beta_two = 0.95
adam_epsilon = 0.3
decay_rate = 0.1
outer_rate = 0.7
outer_momentum = 0.9

MESH = pl.DeviceIdType.MESH
LANES = 128
keep = 1.0 - inner_rate * decay_rate


def flip(index, bit):
    size = 1 << bit
    return index + size * (1 - 2 * (lax.div(index, size) % 2))


def first_update(grad):
    return grad / (jnp.abs(grad) + adam_epsilon)


def second_update(earlier, grad):
    first = (beta_one * (1.0 - beta_one)) * earlier + (1.0 - beta_one) * grad
    second = (beta_two * (1.0 - beta_two)) * earlier * earlier + (1.0 - beta_two) * grad * grad
    first_hat = first * (1.0 / (1.0 - beta_one**2))
    second_hat = second * (1.0 / (1.0 - beta_two**2))
    return first_hat / (jnp.sqrt(second_hat) + adam_epsilon)


def kernel(
    n_i, n_s, low_ref, gain_ref, rows_ref, stream_ref, goals_ref, total_ref, gain_total_ref,
    rows, anchor, later, grads, res, slope_low, stream, goals, from_left, from_right,
    stats, line, gains, gain_moves,
    local_sem, z_send, z_recv, a_send, a_recv, s_send, s_recv, g_send, g_recv, r_send, r_recv,
):
    i = lax.axis_index("island")
    s = lax.axis_index("shard")
    steps, _, block, width = rows.shape
    piece, cols = low_ref.shape
    tokens = n_s * block
    tiles = tokens // LANES
    scale = width ** (-0.5)
    depth = min(512, piece)
    tall = min(256, piece)

    barrier = pltpu.get_barrier_semaphore()
    for d in range(1, n_i):
        pl.semaphore_signal(barrier, inc=1, device_id=(lax.rem(i + d, n_i), s), device_id_type=MESH)
    for d in range(1, n_s):
        pl.semaphore_signal(barrier, inc=1, device_id=(i, lax.rem(s + d, n_s)), device_id_type=MESH)

    locals_ = [pltpu.make_async_copy(low_ref, anchor.at[i], local_sem.at[0])]
    for st in range(steps):
        locals_.append(pltpu.make_async_copy(rows_ref.at[0, st], rows.at[st, s], local_sem.at[1 + st]))
    locals_.append(pltpu.make_async_copy(stream_ref.at[0], stream, local_sem.at[1 + steps]))
    locals_.append(pltpu.make_async_copy(goals_ref.at[0], goals, local_sem.at[2 + steps]))
    for copy in locals_:
        copy.start()
    pl.semaphore_wait(barrier, n_i - 1 + n_s - 1)

    def remote(src, dst, send, recv, to):
        return pltpu.make_async_remote_copy(
            src_ref=src, dst_ref=dst, send_sem=send, recv_sem=recv, device_id=to, device_id_type=MESH
        )

    right, left = (lax.rem(i + 1, n_i), s), (lax.rem(i + n_i - 1, n_i), s)

    def z_copy(way, t, at):
        return remote(
            anchor.at[at], anchor.at[at], z_send.at[way, t], z_recv.at[way, t], right if way == 0 else left
        )

    def z_start(t):
        @pl.when((i < n_i - 1) & (i - t >= 0))
        def _():
            z_copy(0, t, i - t).start()

        @pl.when((i > 0) & (i + t <= n_i - 1))
        def _():
            z_copy(1, t, i + t).start()

    def z_wait(t):
        @pl.when(i - 1 - t >= 0)
        def _():
            z_copy(0, t, i - 1 - t).wait_recv()

        @pl.when(i + 1 + t <= n_i - 1)
        def _():
            z_copy(1, t, i + 1 + t).wait_recv()

    n_bits = n_s.bit_length() - 1
    orders = [list(range(1, n_bits)) + [0], list(range(n_bits - 1, 0, -1)) + [0]]

    def a_blocks(st, phase):
        order = orders[st % 2]
        found = []
        for m in range(1 << phase):
            at = s
            for q in range(phase):
                if (m >> q) & 1:
                    at = flip(at, order[q])
            found.append(at)
        return found

    def a_copy(st, phase, m, at):
        slot = (1 << phase) - 1 + m
        return remote(
            rows.at[st, at], rows.at[st, at], a_send.at[st, slot], a_recv.at[st, slot],
            (i, flip(s, orders[st % 2][phase])),
        )

    def a_start(phase):
        for st in range(steps):
            for m, at in enumerate(a_blocks(st, phase)):
                a_copy(st, phase, m, at).start()

    def a_wait(phase):
        for st in range(steps):
            for m, at in enumerate(a_blocks(st, phase)):
                a_copy(st, phase, m, flip(at, orders[st % 2][phase])).wait_recv()

    def to_islands(buffer, which):
        return [
            remote(
                buffer.at[0], buffer.at[d], g_send.at[which, d], g_recv.at[which, d],
                (lax.rem(i + d, n_i), s),
            )
            for d in range(1, n_i)
        ]

    locals_[0].wait()
    z_start(0)
    for copy in locals_[1 : 1 + steps]:
        copy.wait()
    a_start(0)
    gains[0] = gain_ref[...]
    gain_in = to_islands(gains, 0)
    for copy in gain_in:
        copy.start()
    res[...] = jnp.zeros_like(res)
    for copy in locals_[1 + steps :]:
        copy.wait()

    def project(st, weights, at):
        def body(k, _):
            start = pl.multiple_of(k * depth, depth)
            wide = pl.multiple_of(at * piece + k * depth, depth)
            part = rows[st, :, :, pl.ds(wide, depth)].reshape(tokens, depth)
            res[...] += jnp.dot(part, weights[at, pl.ds(start, depth), :], preferred_element_type=jnp.float32)
            return 0

        lax.fori_loop(0, piece // depth, body, 0)

    def project_arrived(t):
        @pl.when(i - 1 - t >= 0)
        def _():
            project(0, anchor, i - 1 - t)

        @pl.when(i + 1 + t <= n_i - 1)
        def _():
            project(0, anchor, i + 1 + t)

    events = [(2.0 * t + 2.6, "z", t) for t in range(n_i - 1)]
    events += [(2.0 * ((2 << p) - 1), "a", p) for p in range(n_bits - 1)]
    last = events[-1][0] if n_bits > 1 else 0.0
    events.append((last + 0.1, "a", n_bits - 1))
    gathered, ready = False, []
    for _, kind, at in sorted(events):
        if kind == "a":
            a_wait(at)
            if at + 1 < n_bits:
                a_start(at + 1)
            else:
                gathered = True
                project(0, anchor, i)
                for t in ready:
                    project_arrived(t)
        else:
            z_wait(at)
            if at + 1 < n_i - 1:
                z_start(at + 1)
            if gathered:
                project_arrived(at)
            else:
                ready.append(at)

    for copy in gain_in:
        copy.wait()
    gain_anchor = gains[0]
    for d in range(1, n_i):
        gain_anchor = gain_anchor + gains[d]
    gain = gain_anchor

    def fold(value):
        total = value[:, :LANES]
        for c in range(1, cols // LANES):
            total = total + value[:, c * LANES : (c + 1) * LANES]
        return jnp.sum(total.T, axis=0, keepdims=True)

    def spread(value):
        square = jnp.broadcast_to(value, (LANES, LANES)).T
        return jnp.concatenate([square] * (cols // LANES), axis=1)

    def row_stats(st, gain):
        def body(q, _):
            at = pl.ds(pl.multiple_of(q * LANES, LANES), LANES)
            r = stream[st, at, :].astype(jnp.float32) + res[at, :] * scale
            res[at, :] = r
            weighted = r * gain
            stats[st, 0, 0:1, at] = fold(r * r)
            stats[st, 0, 1:2, at] = fold(weighted * weighted)
            stats[st, 0, 2:3, at] = fold(weighted * goals[st, at, :].astype(jnp.float32))
            stats[st, 0, 3:4, at] = jnp.zeros((1, LANES), jnp.float32)
            return 0

        lax.fori_loop(0, tiles, body, 0)
        copies = [
            remote(
                stats.at[st, 0], stats.at[st, d], s_send.at[st, d], s_recv.at[st, d],
                (i, lax.rem(s + d, n_s)),
            )
            for d in range(1, n_s)
        ]
        for copy in copies:
            copy.start()
        for copy in copies:
            copy.wait()
        total = stats[st, 0]
        for d in range(1, n_s):
            total = total + stats[st, d]
        inverse = lax.rsqrt(total[0:1] * (1.0 / width) + norm_epsilon)
        slope = inverse * total[1:2] - total[2:3]
        line[0:1, :] = inverse
        line[1:2, :] = inverse * inverse * inverse * slope * (1.0 / width)

    def row_grads(st, gain):
        def body(q, total):
            at = pl.ds(pl.multiple_of(q * LANES, LANES), LANES)
            inverse, pull = spread(line[0:1, at]), spread(line[1:2, at])
            r = res[at, :]
            unit = r * inverse
            loss = unit * gain - goals[st, at, :].astype(jnp.float32)
            loss = loss.astype(jnp.bfloat16).astype(jnp.float32)
            slope_low[at, :] = (inverse * (loss * gain) - r * pull).astype(jnp.bfloat16)
            return total + jnp.sum(loss * unit, axis=0, keepdims=True)

        return lax.fori_loop(0, tiles, body, jnp.zeros((1, cols), jnp.float32))

    def weight_grad(st, wide):
        part = rows[st, :, :, pl.ds(pl.multiple_of(wide, tall), tall)].reshape(tokens, tall)
        return (
            lax.dot_general(
                part, slope_low[...], (((0,), (0,)), ((), ())), preferred_element_type=jnp.float32
            )
            * scale
        )

    row_stats(0, gain)
    gain_first = row_grads(0, gain)
    per_piece = piece // tall

    def step_one(q, _):
        o, j = q // per_piece, q % per_piece
        at = pl.ds(pl.multiple_of(j * tall, tall), tall)
        grad = weight_grad(0, q * tall)
        grads[o, at, :] = grad
        param = keep * anchor[o, at, :].astype(jnp.float32) - inner_rate * first_update(grad)
        later[o, at, :] = param.astype(jnp.bfloat16)
        return 0

    lax.fori_loop(0, n_i * per_piece, step_one, 0)
    gain_step = first_update(gain_first)
    gain = gain_anchor - inner_rate * gain_step

    res[...] = jnp.zeros_like(res)

    def project_later(at, _):
        project(1, later, at)
        return 0

    lax.fori_loop(0, n_i, project_later, 0)
    row_stats(1, gain)
    gain_second = row_grads(1, gain)
    gain_moves[0] = inner_rate * (gain_step + second_update(gain_first, gain_second))
    gain_out = to_islands(gain_moves, 1)
    for copy in gain_out:
        copy.start()

    def to_right(k):
        at = n_i - 1 - k
        return remote(later.at[at], from_left.at[k], r_send.at[0, k], r_recv.at[0, k], right)

    def to_left(k):
        return remote(later.at[k], from_right.at[k], r_send.at[1, k], r_recv.at[1, k], left)

    order = []
    for k in range((n_i + 1) // 2):
        order += [n_i - 1 - k] + ([k] if k != n_i - 1 - k else [])
    for o in order:

        def step_two(j, _, o=o):
            at = pl.ds(pl.multiple_of(j * tall, tall), tall)
            grad = weight_grad(1, o * piece + j * tall)
            earlier = grads[o, at, :]
            moved = (1.0 - keep * keep) * anchor[o, at, :].astype(jnp.float32) + inner_rate * (
                keep * first_update(earlier) + second_update(earlier, grad)
            )
            grads[o, at, :] = moved
            later[o, at, :] = moved.astype(jnp.bfloat16)
            return 0

        lax.fori_loop(0, per_piece, step_two, 0)
        if o > 0:

            @pl.when(i == 0)
            def _():
                to_right(n_i - 1 - o).start()

        if o < n_i - 1:

            @pl.when(i == n_i - 1)
            def _():
                to_left(o).start()

    def add(o, arrived, k):
        def body(j, _):
            at = pl.ds(pl.multiple_of(j * tall, tall), tall)
            later[o, at, :] = (grads[o, at, :] + arrived[k, at, :].astype(jnp.float32)).astype(jnp.bfloat16)
            return 0

        lax.fori_loop(0, per_piece, body, 0)

    for t in range(n_i - 1):
        k_right = t - i
        k_left = t - (n_i - 1 - i)

        @pl.when((i > 0) & (k_right >= 0) & (k_right < n_i - 1 - i))
        def _():
            to_right(k_right).wait_recv()
            add(n_i - 1 - k_right, from_left, k_right)
            to_right(k_right).start()

        @pl.when((i < n_i - 1) & (k_left >= 0) & (k_left < i))
        def _():
            to_left(k_left).wait_recv()
            add(k_left, from_right, k_left)
            to_left(k_left).start()

    for copy in gain_out:
        copy.wait()
    gain_total = gain_moves[0]
    for d in range(1, n_i):
        gain_total = gain_total + gain_moves[d]
    gain_total_ref[...] = gain_total

    total_ref[...] = grads[i]

    @pl.when(i > 0)
    def _():
        k = n_i - 1 - i
        to_right(k).wait_recv()
        total_ref[...] += from_left[k].astype(jnp.float32)

    @pl.when(i < n_i - 1)
    def _():
        to_left(i).wait_recv()
        total_ref[...] += from_right[i].astype(jnp.float32)

    for k in range(n_i - 1):

        @pl.when(k < n_i - 1 - i)
        def _(k=k):
            to_right(k).wait_send()

        @pl.when(k < i)
        def _(k=k):
            to_left(k).wait_send()

        @pl.when((i < n_i - 1) & (i - k >= 0))
        def _(k=k):
            z_copy(0, k, i - k).wait_send()

        @pl.when((i > 0) & (i + k <= n_i - 1))
        def _(k=k):
            z_copy(1, k, i + k).wait_send()

    for phase in range(n_bits):
        for st in range(steps):
            for m, at in enumerate(a_blocks(st, phase)):
                a_copy(st, phase, m, at).wait_send()


def per_device(weight_master, gain_master, weight_moment, gain_moment, attended, stream, targets):
    n_i, n_s = lax.axis_size("island"), lax.axis_size("shard")
    _, steps, block, width = attended.shape
    _, _, tokens, cols = stream.shape
    piece = weight_master.shape[0]
    own = gain_master.shape[0]
    offset = lax.axis_index("island") * own
    low = weight_master.astype(jnp.bfloat16)
    gain_low = gain_master.astype(jnp.bfloat16).astype(jnp.float32)
    gain_row = lax.dynamic_update_slice(jnp.zeros((1, cols), jnp.float32), gain_low[None], (0, offset))
    any_space = pl.BlockSpec(memory_space=pl.ANY)
    vmem = pl.BlockSpec(memory_space=pltpu.VMEM)
    f32, bf16 = jnp.float32, jnp.bfloat16
    dma = pltpu.SemaphoreType.DMA
    weight_summed, gain_summed = pl.pallas_call(
        functools.partial(kernel, n_i, n_s),
        out_shape=(
            jax.ShapeDtypeStruct((piece, cols), f32),
            jax.ShapeDtypeStruct((1, cols), f32),
        ),
        in_specs=[any_space, vmem, any_space, any_space, any_space],
        out_specs=(vmem, vmem),
        scratch_shapes=[
            pltpu.VMEM((steps, n_s, block, width), bf16),
            pltpu.VMEM((n_i, piece, cols), bf16),
            pltpu.VMEM((n_i, piece, cols), bf16),
            pltpu.VMEM((n_i, piece, cols), f32),
            pltpu.VMEM((tokens, cols), f32),
            pltpu.VMEM((tokens, cols), bf16),
            pltpu.VMEM((steps, tokens, cols), bf16),
            pltpu.VMEM((steps, tokens, cols), bf16),
            pltpu.VMEM((n_i - 1, piece, cols), bf16),
            pltpu.VMEM((n_i - 1, piece, cols), bf16),
            pltpu.VMEM((steps, n_s, 4, tokens), f32),
            pltpu.VMEM((2, tokens), f32),
            pltpu.VMEM((n_i, 1, cols), f32),
            pltpu.VMEM((n_i, 1, cols), f32),
            dma((3 + steps,)),
            dma((2, n_i - 1)),
            dma((2, n_i - 1)),
            dma((steps, n_s - 1)),
            dma((steps, n_s - 1)),
            dma((steps, n_s)),
            dma((steps, n_s)),
            dma((2, n_i)),
            dma((2, n_i)),
            dma((2, n_i - 1)),
            dma((2, n_i - 1)),
        ],
        compiler_params=pltpu.CompilerParams(
            collective_id=0, has_side_effects=True, vmem_limit_bytes=67043328
        ),
    )(low, gain_row, attended, stream, targets)
    weight_pseudo = weight_summed / n_i
    gain_pseudo = lax.dynamic_slice(gain_summed, (0, offset), (1, own))[0] / n_i
    weight_velocity = outer_momentum * weight_moment + weight_pseudo
    gain_velocity = outer_momentum * gain_moment + gain_pseudo
    weight_updated = weight_master - outer_rate * (weight_pseudo + outer_momentum * weight_velocity)
    gain_updated = gain_master - outer_rate * (gain_pseudo + outer_momentum * gain_velocity)
    return (weight_updated, gain_updated, weight_velocity, gain_velocity)


def solution(mesh):
    placed = (
        P("island", "shard"),
        P(("shard", "island")),
        P("island", "shard"),
        P(("shard", "island")),
        P("island", None, "shard", None),
        P("island", None, None, "shard"),
        P("island", None, None, "shard"),
    )
    return jax.shard_map(
        per_device,
        mesh=mesh,
        in_specs=placed,
        out_specs=(
            P("island", "shard"),
            P(("shard", "island")),
            P("island", "shard"),
            P(("shard", "island")),
        ),
        check_vma=False,
    )
```

time: 417 us -> 216 us (0.52)
  waiting for transfers between devices: 233 us -> 0 us
  Pallas kernels: 0 us -> 203 us
  blocking collectives: 70.9 us -> 0 us
  matrix products: 58.1 us -> 0 us
  local copies, waits for them, and re-layouts: 25.8 us -> 0.58 us
  between operations: 14.5 us -> 0.65 us
    pallas_call x0 -> x1, Pallas kernels: none -> 203 us  [per_device(): pl.pallas_call(functools.partial(kernel, n_i, n_s), out_shape=(jax.ShapeD...]
    reduce_scatter x1 -> x0, waiting for transfers between devices: 129 us -> none  [per_device(): lax.psum_scatter(weight_anchor - weight, 'island', scatter_dimension=0, t...]
    all_gather x3 -> x0, waiting for transfers between devices: 103 us -> none  [the longest x1 54.7 us: per_device(): lax.all_gather(weight_master.astype(jnp.bfloat16), 'island', axis=0, tile...]
    dot_general x4 -> x0, matrix products: 58.1 us -> none  [the longest x2 32.8 us: per_device(): jnp.einsum('td,tf->df', rows_full, residual_grad, preferred_element_type=...]
    psum x4 -> x0, blocking collectives: 50.9 us -> none  [the longest x2 26.2 us: per_device(): squares = lax.psum(jnp.sum(residual * residual, axis=1), 'shard')]
    unnamed x25 -> x0, local copies, waits for them, and re-layouts: 18.1 us -> none
    unnamed x1 -> x0, blocking collectives: 11.1 us -> none
    all_gather x1 -> x0, blocking collectives: 8.92 us -> none  [per_device(): lax.all_gather(gain_master.astype(jnp.bfloat16), 'island', axis=0, tiled=...]
  transfers between devices with their start and end apart: 4 -> 0, of which waited for: 3 -> 0; matrix products, arithmetic and copies ran while one was open for 10% -> 0% of each run, Pallas kernels for 0% -> 0%
where the time goes in v1:
time: 216 us; the launch traced here: 215 us
  Pallas kernels  203 us (94%)
  other arithmetic  10.7 us (5%)
    pallas_call x1, Pallas kernels, per_device(): pl.pallas_call(functools.partial(kernel, n_i, n_s), out_shape=(jax.ShapeD...  203 us
    sub x1, other arithmetic, per_device(): weight_master - outer_rate * (weight_pseudo + outer_momentum * weight_vel...  5.66 us

profile of v1, /device:TPU:8, one launch (start us, length us, event | category | flops | bytes accessed | tf_op | source)
XLA Modules:
  0.0 215.3 jit_solution(14513249433053107236)
XLA Ops:
  0.6 0.6 broadcast_in_dim.9
  1.2 1.2 convert_dynamic-update-slice_fusion.gain_ref
  2.4 2.7 %convert_element_type.7.low_ref = bf16[1024,512]{1,0:T(8,128)(2,1)} convert(f32[1024,512]{1,0:T(8,128)} %param.7) | non-fusion elementwise | flops 524288 | bytes 3145728 | tf_op jit(solution)/shard_map/convert_element_type | solution.py:411
  5.1 203.4 %shard_map.102 = (f32[1024,512]{1,0:T(8,128)}, f32[1,512]{1,0:T(1,128)}) custom-call(bf16[1024,512]{1,0:T(8,128)(2,1)} %convert_element_type.7.low_ref, f32[1,512]{1,0:T(1,128)} %convert_dynamic-update-slice_fusion.gain_ref, bf16[1,2,96,4096]{3,2,1,0:T(8,128)(2,1)} %rows_ref.1, bf16[1,2,768,512]{3,2,1,0:T(8,128)(2,1)} %stream_ref.1, ...), custom_call_target="tpu_custom_call" | custom-call | tf_op jit(solution)/shard_map/pallas_call | solution.py:418
  208.5 1.2 fusion.1
  209.7 5.7 %multiply_subtract_fusion = (f32[1024,512]{1,0:T(8,128)}, f32[1024,512]{1,0:T(8,128)}) fusion(f32[1024,512]{1,0:T(8,128)} %param.7, f32[1024,512]{1,0:T(8,128)} %get-tuple-element.6, f32[1024,512]{1,0:T(8,128)} %param.9), kind=kLoop, calls=%fused_computation | loop fusion | flops 3670016 | bytes 10485760 | tf_op jit(solution)/shard_map/sub | solution.py:461

commit v2 on v1

--- a/solution.py
+++ b/solution.py
@@ -304,12 +304,12 @@
     def to_left(k):
         return remote(later.at[k], from_right.at[k], r_send.at[1, k], r_recv.at[1, k], left)
 
-    order = []
-    for k in range((n_i + 1) // 2):
-        order += [n_i - 1 - k] + ([k] if k != n_i - 1 - k else [])
-    for o in order:
-
-        def step_two(j, _, o=o):
+    early = 1 - lax.div(2 * i, n_i)
+
+    def owner_piece(q, _):
+        o = q + early * (n_i - 1 - 2 * q)
+
+        def step_two(j, _):
             at = pl.ds(pl.multiple_of(j * tall, tall), tall)
             grad = weight_grad(1, o * piece + j * tall)
             earlier = grads[o, at, :]
@@ -321,17 +321,18 @@
             return 0
 
         lax.fori_loop(0, per_piece, step_two, 0)
-        if o > 0:
-
-            @pl.when(i == 0)
-            def _():
-                to_right(n_i - 1 - o).start()
-
-        if o < n_i - 1:
-
-            @pl.when(i == n_i - 1)
-            def _():
-                to_left(o).start()
+
+        @pl.when((i == 0) & (o > 0))
+        def _():
+            to_right(n_i - 1 - o).start()
+
+        @pl.when((i == n_i - 1) & (o < n_i - 1))
+        def _():
+            to_left(o).start()
+
+        return 0
+
+    lax.fori_loop(0, n_i, owner_piece, 0)
 
     def add(o, arrived, k):
         def body(j, _):

time: 216 us -> 192 us (0.89)
  Pallas kernels: 203 us -> 179 us
    pallas_call x1, Pallas kernels: 203 us -> 179 us  [per_device(): pl.pallas_call(functools.partial(kernel, n_i, n_s), out_shape=(jax.ShapeD...]
where the time goes in v2:
time: 192 us; the launch traced here: 191 us
  Pallas kernels  179 us (93%)
  other arithmetic  10.7 us (6%)
    pallas_call x1, Pallas kernels, per_device(): pl.pallas_call(functools.partial(kernel, n_i, n_s), out_shape=(jax.ShapeD...  179 us
    sub x1, other arithmetic, per_device(): weight_master - outer_rate * (weight_pseudo + outer_momentum * weight_vel...  5.66 us

profile of v2, /device:TPU:8, one launch (start us, length us, event | category | flops | bytes accessed | tf_op | source)
XLA Modules:
  0.0 190.5 jit_solution(14386328629131301467)
XLA Ops:
  0.6 0.6 broadcast_in_dim.9
  1.2 1.2 convert_dynamic-update-slice_fusion.gain_ref
  2.4 2.7 %convert_element_type.7.low_ref = bf16[1024,512]{1,0:T(8,128)(2,1)} convert(f32[1024,512]{1,0:T(8,128)} %param.7) | non-fusion elementwise | flops 524288 | bytes 3145728 | tf_op jit(solution)/shard_map/convert_element_type | solution.py:412
  5.1 178.6 %shard_map.102 = (f32[1024,512]{1,0:T(8,128)}, f32[1,512]{1,0:T(1,128)}) custom-call(bf16[1024,512]{1,0:T(8,128)(2,1)} %convert_element_type.7.low_ref, f32[1,512]{1,0:T(1,128)} %convert_dynamic-update-slice_fusion.gain_ref, bf16[1,2,96,4096]{3,2,1,0:T(8,128)(2,1)} %rows_ref.1, bf16[1,2,768,512]{3,2,1,0:T(8,128)(2,1)} %stream_ref.1, ...), custom_call_target="tpu_custom_call" | custom-call | tf_op jit(solution)/shard_map/pallas_call | solution.py:419
  183.6 1.2 fusion.1
  184.8 5.7 %multiply_subtract_fusion = (f32[1024,512]{1,0:T(8,128)}, f32[1024,512]{1,0:T(8,128)}) fusion(f32[1024,512]{1,0:T(8,128)} %param.7, f32[1024,512]{1,0:T(8,128)} %get-tuple-element.6, f32[1024,512]{1,0:T(8,128)} %param.9), kind=kLoop, calls=%fused_computation | loop fusion | flops 3670016 | bytes 10485760 | tf_op jit(solution)/shard_map/sub | solution.py:462
